TPU v7x, 32 devices: a whole 2x2x4 slice. The times are simulated.
32 devices in a mesh: row: 4 (over z), col: 8 (over y, x, core).
Axes of the slice: x: 2, y: 2, z: 4, core: 2. Of those that a mesh axis runs over, the one named last changes fastest.
Arguments:
- points: float32 [131072, 64], P(('row', 'col')), may hold values from -6 to 6
- factor: float32 [131072, 512], P(('row', 'col')), may hold values from -0.06 to 0.06
- pivots: int32 [2, 128], replicated, may hold values from 0 to 131071, as said below
Outputs:
- factor_new: float32 [131072, 256], P(('row', 'col'))
- gram_rows: float32 [256, 768], replicated
Inputs may be any that keep to these rules, and one draw needn't show every extreme that they name: All 256 pivots are different points.
All inputs are finite; a program needn't handle non-finite values.
Results may differ from a plain program's by a relative error of at most 0.00013.
Values sent between devices are 32-bit elements; how exact they have to be, the bound alone decides.
No kernel may reach another device: no remote copies, remote signals or barrier semaphores. Data moves between devices by JAX's collectives and lax.ppermute only.
A program may use at most 128 MiB of HBM per device.

v0:
```python
import jax
import jax.numpy as jnp
from jax import lax
from jax.sharding import PartitionSpec as P

highest = lax.Precision.HIGHEST
nugget = 0.1


def kernel_block(left, right):
    cross = jnp.dot(left, right.T, precision=highest)
    dist = jnp.sum(left * left, 1)[:, None] + jnp.sum(right * right, 1)[None, :] - 2.0 * cross
    return jnp.exp(-dist / left.shape[1])


def pivot_inverse(pivot_points, pivot_factor):
    size = pivot_points.shape[0]
    identity = jnp.eye(size, dtype=jnp.float32)
    outer = jnp.dot(pivot_factor, pivot_factor.T, precision=highest)
    shift = nugget + jnp.max(jnp.sum(jnp.abs(outer), 1))
    core = kernel_block(pivot_points, pivot_points) - outer + shift * identity
    lower = jnp.linalg.cholesky(core)
    return jax.scipy.linalg.solve_triangular(lower, identity, lower=True)


def new_columns(rows_points, rows_factor, pivot_points, pivot_factor, inverse):
    resid = kernel_block(rows_points, pivot_points) - jnp.dot(
        rows_factor, pivot_factor.T, precision=highest
    )
    return jnp.dot(resid, inverse.T, precision=highest)


def pick_rows(table, indices, offset, count):
    local = indices - offset
    inside = (local >= 0) & (local < count)
    taken = jnp.take(table, jnp.clip(local, 0, count - 1), axis=0)
    return jnp.where(inside[:, None], taken, jnp.zeros_like(taken))


def body(points, factor, pivots):
    count = points.shape[0]
    width = points.shape[1]
    size = pivots.shape[1]
    offset = (lax.axis_index("row") * lax.axis_size("col") + lax.axis_index("col")) * count
    current = factor
    made = []
    local_rows = pick_rows(jnp.concatenate([points, factor], 1), pivots.reshape(-1), offset, count)
    fetched = lax.psum(local_rows, ("row", "col"))
    all_points = fetched[:, :width]
    all_factor = fetched[:, width:]
    for section in range(pivots.shape[0]):
        pivot_points = all_points[section * size : (section + 1) * size]
        pivot_factor = all_factor[section * size : (section + 1) * size]
        inverse = pivot_inverse(pivot_points, pivot_factor)
        fresh = new_columns(points, current, pivot_points, pivot_factor, inverse)
        at_pivots = new_columns(all_points, all_factor, pivot_points, pivot_factor, inverse)
        all_factor = jnp.concatenate([all_factor, at_pivots], 1)
        made.append(fresh)
        current = jnp.concatenate([current, fresh], 1)
    factor_new = jnp.concatenate(made, 1)
    terms = jnp.dot(factor_new.T, current, precision=highest)
    total = lax.psum(terms, ("row", "col"))
    return (factor_new, total / count)


def solution(mesh):
    in_specs = (P(("row", "col"), None), P(("row", "col"), None), P())
    out_specs = (P(("row", "col"), None), P())
    return jax.shard_map(body, mesh=mesh, in_specs=in_specs, out_specs=out_specs, check_vma=False)
```

profile of v0, /device:TPU:0, one launch (start us, length us, event | category | flops | bytes accessed | tf_op | source)
XLA Modules:
  0.0 412.9 jit_solution(3661174679678323361)
XLA Ops:
  7.2 0.0 all-reduce.3.cloned.1.call-start
  7.2 0.7 compare_and_fusion
  7.9 0.7 and_bitcast_fusion
  8.6 1.8 copy.5
  10.4 10.1 %pad_maximum_fusion = f32[4096,576]{1,0:T(8,128)} fusion(f32[4096,512]{1,0:T(8,128)} %param.7, f32[4096,64]{1,0:T(8,128)S(1)} %copy.5), kind=kLoop, calls=%fused_computation.7 | loop fusion | flops 2359296 | bytes 18874368 | tf_op jit(solution)/shard_map/concatenate | solution.py:47
  20.6 5.3 %gather_fusion = f32[256,576]{1,0:T(8,128)S(1)} fusion(f32[4096,576]{1,0:T(8,128)} %pad_maximum_fusion, s32[1024]{0:T(1024)S(1)} %pad_clamp_fusion), kind=kCustom, calls=%fused_computation | custom fusion | bytes 1180672 | tf_op jit(solution)/shard_map/jit(_take)/gather | solution.py:36
  25.8 0.0 copy-start
  25.9 1.0 select_select_fusion
  26.8 0.0 all-reduce.3.cloned.1.call-update
  26.9 0.3 all-reduce.5.cloned.1.call-start
  27.2 0.1 copy-done
  27.3 0.1 multiply_reduce_fusion
  27.4 131.9 %all-reduce.3.cloned.1.call-done = f32[256,576]{1,0:T(8,128)} async-done(((f32[256,576]{1,0:T(8,128)}), f32[256,576]{1,0:T(8,128)}) %all-reduce.3.cloned.1.call-update) | async-done | bytes 589840 | tf_op jit(solution)/shard_map/psum | solution.py:48
  159.4 0.0 copy-start.1
  159.4 1.6 abs_reduce_fusion.1
  161.0 0.6 reduce_max.18
  162.2 1.0 multiply_reduce_fusion.2
  163.2 1.2 fusion.35
  164.4 0.1 copy.7
  164.6 11.7 %cholesky.44 = f32[128,128]{1,0:T(8,128)S(1)} custom-call(f32[128,128]{1,0:T(8,128)S(1)} %fusion.53), custom_call_target="Cholesky" | custom-call | tf_op jit(solution)/shard_map/jit(cholesky)/cholesky | solution.py:22
  176.3 0.6 compare_reduce_fusion.1
  176.9 0.7 fusion.48
  177.6 9.8 %custom-call.6 = f32[1,128,128]{1,2,0:T(8,128)S(1)} custom-call(f32[1,128,128]{2,1,0:T(8,128)S(1)} %fusion.48), custom_call_target="InvertDiagBlocksLowerTriangular" | custom-call | tf_op jit(solution)/shard_map/jit(_solve_triangular)/triangular_solve | solution.py:23
  187.4 0.3 fusion.46
  187.7 1.0 multiply_reduce_fusion.1
  188.7 1.2 fusion.25
  189.9 0.0 copy-done.1
  190.0 0.7 convolution_subtract_fusion
  190.6 0.3 fusion.64
  190.9 0.2 slice.40
  191.1 0.0 copy-start.2
  191.1 0.5 abs_reduce_fusion
  191.6 0.6 reduce_max.19
  192.9 0.3 fusion.37
  193.2 0.1 copy.11
  193.3 12.2 %cholesky.55 = f32[128,128]{1,0:T(8,128)S(1)} custom-call(f32[128,128]{1,0:T(8,128)S(1)} %fusion.51), custom_call_target="Cholesky" | custom-call | tf_op jit(solution)/shard_map/jit(cholesky)/cholesky | solution.py:22
  205.5 0.6 compare_reduce_fusion
  206.2 0.7 fusion.49
  206.8 9.8 %custom-call.7 = f32[1,128,128]{1,2,0:T(8,128)S(1)} custom-call(f32[1,128,128]{2,1,0:T(8,128)S(1)} %fusion.49), custom_call_target="InvertDiagBlocksLowerTriangular" | custom-call | tf_op jit(solution)/shard_map/jit(_solve_triangular)/triangular_solve | solution.py:23
  216.6 0.3 fusion.44
  216.9 3.9 fusion.21
  220.8 0.0 copy-done.2
  220.8 9.4 %fusion.16 = f32[4096,128]{1,0:T(8,128)S(1)} fusion(f32[4096,128]{1,0:T(8,128)S(1)} %fusion.21, f32[4096,512]{1,0:T(8,128)} %param.7, f32[256,576]{1,0:T(8,128)S(1)} %copy-done.1), kind=kOutput, calls=%fused_computation.20 | convolution fusion | flops 3221749760 | bytes 12845056 | tf_op jit(solution)/shard_map/dot_general | solution.py:27
  230.2 2.0 fusion.63
  232.2 1.8 copy.8
  234.1 11.5 %fusion.6 = f32[4096,128]{1,0:T(8,128)S(1)} fusion(f32[4096,128]{1,0:T(8,128)} %copy.8, f32[4096,512]{1,0:T(8,128)} %param.7, f32[256,128]{1,0:T(8,128)S(1)} %fusion.64, f32[256,512]{1,0:T(8,128)} %copy-done.2), kind=kOutput, calls=%fused_computation.8 | convolution fusion | flops 4029235200 | bytes 13238272 | tf_op jit(solution)/shard_map/dot_general | solution.py:27
  245.6 4.9 %fusion.15 = f32[4096,128]{1,0:T(8,128)S(1)} fusion(f32[4096,128]{1,0:T(8,128)S(1)} %fusion.6, f32[4096,64]{0,1:T(8,128)S(1)} %copy-done, f32[128]{0:T(128)S(1)} %get-tuple-element.6, f32[4096]{0:T(1024)S(1)} %multiply_reduce_fusion, f32[256,576]{1,0:T(8,128)} %all-reduce.3.cloned.1.call-done), kind=kOutput, calls=%fused_computation.18 | convolution fusion | flops 405798912 | bytes 5325312 | tf_op jit(solution)/shard_map/dot_general | solution.py:11
  250.5 3.3 fusion.65
  253.8 2.9 copy.13
  256.7 18.0 %fusion = f32[256,768]{1,0:T(8,128)} fusion(f32[4096,128]{1,0:T(8,128)} %copy.13, f32[4096,128]{1,0:T(8,128)} %copy.8, f32[4096,512]{1,0:T(8,128)} %param.7, f32[4096,128]{0,1:T(8,128)} %fusion.65, f32[4096,128]{0,1:T(8,128)S(1)} %fusion.63), kind=kOutput, calls=%fused_computation.1 | convolution fusion | flops 9671016448 | bytes 17563648 | tf_op jit(solution)/shard_map/dot_general | solution.py:61
  274.7 0.0 all-reduce.5.cloned.1.call-update
  274.8 3.9 pad_maximum_fusion.1
  278.7 5.6 %copy.14 = f32[4096,256]{1,0:T(8,128)} copy(f32[4096,256]{0,1:T(8,128)} %pad_maximum_fusion.1) | data formatting | bytes 8388608
  284.3 119.4 %all-reduce.5.cloned.1.call-done = f32[256,768]{1,0:T(8,128)} async-done(((f32[256,768]{1,0:T(8,128)}), f32[256,768]{1,0:T(8,128)}) %all-reduce.5.cloned.1.call-update) | async-done | bytes 786448 | tf_op jit(solution)/shard_map/psum | solution.py:62
  403.7 2.1 broadcast_multiply_fusion
  (6 shorter events, 0.1 us)
Async XLA Ops:
  7.2 152.2 %all-reduce.3.cloned.1.call-start = ((), (), s32[]{:S(2)}) async-start(), calls=%async_computation | async-start | bytes 1310720 | tf_op jit(solution)/shard_map/psum | solution.py:48
  25.8 1.5 copy-start
  26.9 376.9 %all-reduce.5.cloned.1.call-start = ((), (), s32[]{:S(2)}) async-start(), calls=%async_computation.1 | async-start | bytes 1572864 | tf_op jit(solution)/shard_map/psum | solution.py:62
  159.4 30.6 %copy-start.1 = (f32[256,576]{1,0:T(8,128)S(1)}, f32[256,576]{1,0:T(8,128)}, u32[]{:S(2)}) copy-start(f32[256,576]{1,0:T(8,128)} %all-reduce.3.cloned.1.call-done) | copy-start | bytes 1769476
  191.1 29.7 %copy-start.2 = (f32[256,512]{1,0:T(8,128)}, f32[256,512]{1,0:T(8,128)S(1)}, u32[]{:S(2)}) copy-start(f32[256,512]{1,0:T(8,128)S(1)} %slice.40) | copy-start | bytes 1572868
Sparse Core Ops, SparseCore 0:
  27.0 132.3 all-reduce.2
  274.9 128.8 all-reduce.4
where the time goes:
time: 417 us; the launch traced here: 413 us
  waiting for transfers between devices  251 us (60%)
  other arithmetic  68 us (16%)
  matrix products  59.3 us (14%)
  local copies, waits for them, and re-layouts  18 us (4%)
  between operations  15.8 us (4%)
    psum x1, waiting for transfers between devices, body(): fetched = lax.psum(local_rows, ('row', 'col'))  132 us
    psum x1, waiting for transfers between devices, body(): total = lax.psum(terms, ('row', 'col'))  119 us
    another operation x6, other arithmetic, pivot_inverse(): lower = jnp.linalg.cholesky(core)  25.2 us
    dot_general x3, matrix products, new_columns(): jnp.dot(rows_factor, pivot_factor.T, precision=highest)  21.6 us
    another operation x4, other arithmetic, pivot_inverse(): return jax.scipy.linalg.solve_triangular(lower, identity, lower=True)  20.9 us
    dot_general x1, matrix products, body(): terms = jnp.dot(factor_new.T, current, precision=highest)  18 us
    dot_general x5, matrix products, kernel_block(): cross = jnp.dot(left, right.T, precision=highest)  11.4 us
    concatenate x1, other arithmetic, body(): jnp.concatenate([points, factor], 1)  10.1 us
  transfers between devices with their start and end apart: 2, of which 2 were waited for; matrix products, arithmetic and copies ran while one was open for 2% of the time, Pallas kernels for 0%

commit v1 on v0

--- a/solution.py
+++ b/solution.py
@@ -59,7 +59,9 @@
         current = jnp.concatenate([current, fresh], 1)
     factor_new = jnp.concatenate(made, 1)
     terms = jnp.dot(factor_new.T, current, precision=highest)
-    total = lax.psum(terms, ("row", "col"))
+    total = terms
+    for over in ("col", "row"):
+        total = lax.psum(total, over)
     return (factor_new, total / count)
 
 

time: 417 us -> 388 us (0.930)
  waiting for transfers between devices: 251 us -> 223 us
    psum x1 -> x2, waiting for transfers between devices: 119 us -> 90.8 us  [body(): total = lax.psum(total, over)]
  transfers between devices with their start and end apart: 2 -> 3, of which waited for: 2 -> 3; matrix products, arithmetic and copies ran while one was open for 2% -> 3% of each run, Pallas kernels for 0% -> 0%
where the time goes in v1:
time: 388 us; the launch traced here: 384 us
  waiting for transfers between devices  223 us (57%)
  other arithmetic  68 us (18%)
  matrix products  59.3 us (15%)
  local copies, waits for them, and re-layouts  18 us (5%)
  between operations  15.5 us (4%)
    psum x1, waiting for transfers between devices, body(): fetched = lax.psum(local_rows, ('row', 'col'))  132 us
    psum x2, waiting for transfers between devices, body(): total = lax.psum(total, over)  90.8 us
    another operation x6, other arithmetic, pivot_inverse(): lower = jnp.linalg.cholesky(core)  25.2 us
    dot_general x3, matrix products, new_columns(): jnp.dot(rows_factor, pivot_factor.T, precision=highest)  21.6 us
    another operation x4, other arithmetic, pivot_inverse(): return jax.scipy.linalg.solve_triangular(lower, identity, lower=True)  20.9 us
    dot_general x1, matrix products, body(): terms = jnp.dot(factor_new.T, current, precision=highest)  18 us
    dot_general x5, matrix products, kernel_block(): cross = jnp.dot(left, right.T, precision=highest)  11.4 us
    concatenate x1, other arithmetic, body(): jnp.concatenate([points, factor], 1)  10.1 us
  transfers between devices with their start and end apart: 3, of which 3 were waited for; matrix products, arithmetic and copies ran while one was open for 3% of the time, Pallas kernels for 0%

profile of v1, /device:TPU:0, one launch (start us, length us, event | category | flops | bytes accessed | tf_op | source)
XLA Modules:
  0.0 384.0 jit_solution(12459187002654492945)
XLA Ops:
  7.2 0.0 all-reduce.4.cloned.1.call-start
  7.2 0.7 compare_and_fusion
  7.9 0.7 and_bitcast_fusion
  8.6 1.8 copy.5
  10.4 10.1 %pad_maximum_fusion = f32[4096,576]{1,0:T(8,128)} fusion(f32[4096,512]{1,0:T(8,128)} %param.7, f32[4096,64]{1,0:T(8,128)S(1)} %copy.5), kind=kLoop, calls=%fused_computation.7 | loop fusion | flops 2359296 | bytes 18874368 | tf_op jit(solution)/shard_map/concatenate | solution.py:47
  20.6 5.3 %gather_fusion = f32[256,576]{1,0:T(8,128)S(1)} fusion(f32[4096,576]{1,0:T(8,128)} %pad_maximum_fusion, s32[1024]{0:T(1024)S(1)} %pad_clamp_fusion), kind=kCustom, calls=%fused_computation | custom fusion | bytes 1180672 | tf_op jit(solution)/shard_map/jit(_take)/gather | solution.py:36
  25.8 0.0 copy-start
  25.9 1.0 select_select_fusion
  26.8 0.0 all-reduce.4.cloned.1.call-update
  26.9 0.3 all-reduce.6.cloned.1.call-start
  27.2 0.1 copy-done
  27.3 0.1 multiply_reduce_fusion
  27.4 131.9 %all-reduce.4.cloned.1.call-done = f32[256,576]{1,0:T(8,128)} async-done(((f32[256,576]{1,0:T(8,128)}), f32[256,576]{1,0:T(8,128)}) %all-reduce.4.cloned.1.call-update) | async-done | bytes 589840 | tf_op jit(solution)/shard_map/psum | solution.py:48
  159.4 0.0 copy-start.1
  159.4 1.6 abs_reduce_fusion.1
  161.0 0.6 reduce_max.18
  162.2 1.0 multiply_reduce_fusion.2
  163.2 1.2 fusion.35
  164.4 0.1 copy.7
  164.6 11.7 %cholesky.44 = f32[128,128]{1,0:T(8,128)S(1)} custom-call(f32[128,128]{1,0:T(8,128)S(1)} %fusion.53), custom_call_target="Cholesky" | custom-call | tf_op jit(solution)/shard_map/jit(cholesky)/cholesky | solution.py:22
  176.3 0.6 compare_reduce_fusion.1
  176.9 0.7 fusion.48
  177.6 9.8 %custom-call.6 = f32[1,128,128]{1,2,0:T(8,128)S(1)} custom-call(f32[1,128,128]{2,1,0:T(8,128)S(1)} %fusion.48), custom_call_target="InvertDiagBlocksLowerTriangular" | custom-call | tf_op jit(solution)/shard_map/jit(_solve_triangular)/triangular_solve | solution.py:23
  187.4 0.3 fusion.46
  187.7 1.0 multiply_reduce_fusion.1
  188.7 1.2 fusion.25
  189.9 0.0 copy-done.1
  190.0 0.7 convolution_subtract_fusion
  190.6 0.3 fusion.64
  190.9 0.2 slice.40
  191.1 0.0 copy-start.2
  191.1 0.5 abs_reduce_fusion
  191.6 0.6 reduce_max.19
  192.9 0.3 fusion.37
  193.2 0.1 copy.11
  193.3 12.2 %cholesky.55 = f32[128,128]{1,0:T(8,128)S(1)} custom-call(f32[128,128]{1,0:T(8,128)S(1)} %fusion.51), custom_call_target="Cholesky" | custom-call | tf_op jit(solution)/shard_map/jit(cholesky)/cholesky | solution.py:22
  205.5 0.6 compare_reduce_fusion
  206.2 0.7 fusion.49
  206.8 9.8 %custom-call.7 = f32[1,128,128]{1,2,0:T(8,128)S(1)} custom-call(f32[1,128,128]{2,1,0:T(8,128)S(1)} %fusion.49), custom_call_target="InvertDiagBlocksLowerTriangular" | custom-call | tf_op jit(solution)/shard_map/jit(_solve_triangular)/triangular_solve | solution.py:23
  216.6 0.3 fusion.44
  216.9 3.9 %fusion.21 = f32[4096,128]{1,0:T(8,128)S(1)} fusion(f32[4096,64]{0,1:T(8,128)S(1)} %copy-done, f32[128]{0:T(128)S(1)} %get-tuple-element.7, f32[4096]{0:T(1024)S(1)} %multiply_reduce_fusion, f32[256,576]{1,0:T(8,128)S(1)} %copy-done.1), kind=kOutput, calls=%fused_computation.26 | convolution fusion | flops 405274624 | bytes 3228160 | tf_op jit(solution)/shard_map/dot_general | solution.py:11
  220.8 0.0 copy-done.2
  220.8 9.4 %fusion.16 = f32[4096,128]{1,0:T(8,128)S(1)} fusion(f32[4096,128]{1,0:T(8,128)S(1)} %fusion.21, f32[4096,512]{1,0:T(8,128)} %param.7, f32[256,576]{1,0:T(8,128)S(1)} %copy-done.1), kind=kOutput, calls=%fused_computation.20 | convolution fusion | flops 3221749760 | bytes 12845056 | tf_op jit(solution)/shard_map/dot_general | solution.py:27
  230.2 2.0 fusion.63
  232.2 1.8 copy.8
  234.1 11.5 %fusion.6 = f32[4096,128]{1,0:T(8,128)S(1)} fusion(f32[4096,128]{1,0:T(8,128)} %copy.8, f32[4096,512]{1,0:T(8,128)} %param.7, f32[256,128]{1,0:T(8,128)S(1)} %fusion.64, f32[256,512]{1,0:T(8,128)} %copy-done.2), kind=kOutput, calls=%fused_computation.8 | convolution fusion | flops 4029235200 | bytes 13238272 | tf_op jit(solution)/shard_map/dot_general | solution.py:27
  245.6 4.9 %fusion.15 = f32[4096,128]{1,0:T(8,128)S(1)} fusion(f32[4096,128]{1,0:T(8,128)S(1)} %fusion.6, f32[4096,64]{0,1:T(8,128)S(1)} %copy-done, f32[128]{0:T(128)S(1)} %get-tuple-element.6, f32[4096]{0:T(1024)S(1)} %multiply_reduce_fusion, f32[256,576]{1,0:T(8,128)} %all-reduce.4.cloned.1.call-done), kind=kOutput, calls=%fused_computation.18 | convolution fusion | flops 405798912 | bytes 5325312 | tf_op jit(solution)/shard_map/dot_general | solution.py:11
  250.5 3.3 fusion.65
  253.8 2.9 copy.13
  256.7 18.0 %fusion = f32[256,768]{1,0:T(8,128)} fusion(f32[4096,128]{1,0:T(8,128)} %copy.13, f32[4096,128]{1,0:T(8,128)} %copy.8, f32[4096,512]{1,0:T(8,128)} %param.7, f32[4096,128]{0,1:T(8,128)} %fusion.65, f32[4096,128]{0,1:T(8,128)S(1)} %fusion.63), kind=kOutput, calls=%fused_computation.1 | convolution fusion | flops 9671016448 | bytes 17563648 | tf_op jit(solution)/shard_map/dot_general | solution.py:61
  274.7 0.0 all-reduce.6.cloned.1.call-update
  274.8 0.0 all-reduce.8.cloned.1.call-start
  274.8 54.8 %all-reduce.6.cloned.1.call-done = f32[256,768]{1,0:T(8,128)} async-done(((f32[256,768]{1,0:T(8,128)}), f32[256,768]{1,0:T(8,128)}) %all-reduce.6.cloned.1.call-update) | async-done | bytes 786448 | tf_op jit(solution)/shard_map/psum | solution.py:64
  329.6 0.0 all-reduce.8.cloned.1.call-update
  329.6 3.9 %pad_maximum_fusion.1 = f32[4096,256]{0,1:T(8,128)} fusion(f32[4096,128]{0,1:T(8,128)} %fusion.65, f32[4096,128]{0,1:T(8,128)S(1)} %fusion.63), kind=kLoop, calls=%fused_computation.27 | loop fusion | flops 1048576 | bytes 8388608 | tf_op jit(solution)/shard_map/concatenate | solution.py:60
  333.5 5.6 %copy.14 = f32[4096,256]{1,0:T(8,128)} copy(f32[4096,256]{0,1:T(8,128)} %pad_maximum_fusion.1) | data formatting | bytes 8388608
  339.1 36.0 %all-reduce.8.cloned.1.call-done = f32[256,768]{1,0:T(8,128)} async-done(((f32[256,768]{1,0:T(8,128)}), f32[256,768]{1,0:T(8,128)}) %all-reduce.8.cloned.1.call-update) | async-done | bytes 786448 | tf_op jit(solution)/shard_map/psum | solution.py:64
  375.2 2.1 broadcast_multiply_fusion
  (6 shorter events, 0.1 us)
Async XLA Ops:
  7.2 152.2 %all-reduce.4.cloned.1.call-start = ((), (), s32[]{:S(2)}) async-start(), calls=%async_computation | async-start | bytes 1310720 | tf_op jit(solution)/shard_map/psum | solution.py:48
  25.8 1.5 copy-start
  26.9 302.7 %all-reduce.6.cloned.1.call-start = ((), (), s32[]{:S(2)}) async-start(), calls=%async_computation.1 | async-start | bytes 1572864 | tf_op jit(solution)/shard_map/psum | solution.py:64
  159.4 30.6 %copy-start.1 = (f32[256,576]{1,0:T(8,128)S(1)}, f32[256,576]{1,0:T(8,128)}, u32[]{:S(2)}) copy-start(f32[256,576]{1,0:T(8,128)} %all-reduce.4.cloned.1.call-done) | copy-start | bytes 1769476
  191.1 29.7 %copy-start.2 = (f32[256,512]{1,0:T(8,128)}, f32[256,512]{1,0:T(8,128)S(1)}, u32[]{:S(2)}) copy-start(f32[256,512]{1,0:T(8,128)S(1)} %slice.40) | copy-start | bytes 1572868
  274.8 100.4 %all-reduce.8.cloned.1.call-start = ((), (), s32[]{:S(2)}) async-start(), calls=%async_computation.2 | async-start | bytes 1572864 | tf_op jit(solution)/shard_map/psum | solution.py:64
Sparse Core Ops, SparseCore 0:
  27.0 132.3 all-reduce.3
  274.9 54.6 all-reduce.5
  332.0 43.1 all-reduce.7
